TPU v7x, 32 devices: a whole 2x2x4 slice. The times are simulated.
32 devices in a mesh: kpt: 2 (over x), row: 8 (over z, y), col: 2 (over core).
Axes of the slice: x: 2, y: 2, z: 4, core: 2. Of those that a mesh axis runs over, the one named last changes fastest.
Arguments:
- wannier: float32 [64, 32, 1024], P('kpt', ('row', 'col')), parts along dimension 0, may hold values from -6 to 6
- pairs: int32 [384, 2], replicated, may hold values from 0 to 31, as said below
- gmap: int32 [8192], replicated, may hold values from 1 to 32767, as said below
- screened: bfloat16 [4, 2, 8192, 8192], P('kpt', None, 'row', 'col'), parts along dimension 0, may hold values from -0.046875 to 0.046875
Outputs:
- coulomb: float32 [2, 2, 768, 384], P(None, None, ('kpt', 'row', 'col')), parts along dimension 2
There are 2 independent parts, one for each index of `kpt`. A program takes and returns all parts, laid end to end along the dimension named above; an argument that names none is the same for every part. Nothing has to cross between parts.
Inputs may be any that keep to these rules, and one draw needn't show every extreme that they name: `gmap`: 8192 distinct flat cells of the grid; cell 0 is never among them. `pairs`: in each row the first Wannier function is no greater than the second; no two rows are equal.
All inputs are finite; a program needn't handle non-finite values.
Results may differ from a plain program's by a relative error of at most 0.0082.
Values may be sent and summed in bfloat16 or wider, within the bound.
No kernel may reach another device: no remote copies, remote signals or barrier semaphores. Data moves between devices by JAX's collectives and lax.ppermute only.
A program may use at most 128 MiB of HBM per device.

v0:
```python
import math
import jax
import jax.numpy as jnp
from jax import lax
from jax.sharding import PartitionSpec as P

NW = 32
GX = 32
NG = 8192
NP = 384


def line_tables(side_len):
    positions = jnp.arange(side_len, dtype=jnp.int32)
    phase_index = positions[:, None] * positions[None, :] % side_len
    angles = phase_index.astype(jnp.float32) * (2.0 * math.pi / side_len)
    return (jnp.cos(angles), jnp.sin(angles))


def plane_transform(density):
    cosine, sine_table = line_tables(GX)
    highest = lax.Precision.HIGHEST
    shaped = density.reshape(-1, GX, GX)
    real_z = jnp.einsum("nyz,kz->nyk", shaped, cosine, precision=highest)
    imag_z = -jnp.einsum("nyz,kz->nyk", shaped, sine_table, precision=highest)
    new_real = jnp.einsum("jy,nyk->njk", cosine, real_z, precision=highest) + jnp.einsum(
        "jy,nyk->njk", sine_table, imag_z, precision=highest
    )
    new_imag = jnp.einsum("jy,nyk->njk", cosine, imag_z, precision=highest) - jnp.einsum(
        "jy,nyk->njk", sine_table, real_z, precision=highest
    )
    return (new_real.reshape(density.shape), new_imag.reshape(density.shape))


def line_transform(real_part, imag_part):
    cosine, sine_table = line_tables(GX)
    highest = lax.Precision.HIGHEST
    new_real = jnp.einsum("kn,pny->pky", cosine, real_part, precision=highest) + jnp.einsum(
        "kn,pny->pky", sine_table, imag_part, precision=highest
    )
    new_imag = jnp.einsum("kn,pny->pky", cosine, imag_part, precision=highest) - jnp.einsum(
        "kn,pny->pky", sine_table, real_part, precision=highest
    )
    return (new_real, new_imag)


def right_columns(screened, segment):
    w_real = screened[:, 0]
    w_imag = screened[:, 1]
    real_real = jnp.einsum("fgh,bh->fgb", w_real, segment[0], preferred_element_type=jnp.float32)
    imag_imag = jnp.einsum("fgh,bh->fgb", w_imag, segment[1], preferred_element_type=jnp.float32)
    real_imag = jnp.einsum("fgh,bh->fgb", w_real, segment[1], preferred_element_type=jnp.float32)
    imag_real = jnp.einsum("fgh,bh->fgb", w_imag, segment[0], preferred_element_type=jnp.float32)
    return jnp.stack([real_real - imag_imag, real_imag + imag_real], axis=1)


def shards(wannier, pairs, gmap, screened):
    planes = wannier.shape[1]
    grid_cells = wannier.shape[2]
    members = jnp.arange(NW, dtype=jnp.int32)[None, :]
    pick_first = (pairs[:, 0:1] == members).astype(jnp.float32)
    pick_second = (pairs[:, 1:2] == members).astype(jnp.float32)
    flat_rows = wannier.reshape(NW, -1)
    highest = lax.Precision.HIGHEST
    density = jnp.dot(pick_first, flat_rows, precision=highest) * jnp.dot(
        pick_second, flat_rows, precision=highest
    )
    density = density.reshape(NP, planes, grid_cells)
    arrived = lax.all_to_all(density, ("row", "col"), split_axis=0, concat_axis=1, tiled=True)
    real_part, imag_part = plane_transform(arrived)
    real_part, imag_part = line_transform(real_part, imag_part)
    owned = real_part.shape[0]
    norm_factor = 1.0 / math.sqrt(GX * GX * GX)
    rho_real = jnp.take(real_part.reshape(owned, -1), gmap, axis=1) * norm_factor
    rho_imag = jnp.take(imag_part.reshape(owned, -1), gmap, axis=1) * norm_factor
    rho = jnp.stack([rho_real, rho_imag], axis=0).astype(jnp.bfloat16)
    row_span = screened.shape[2]
    halves = lax.all_to_all(rho, "col", split_axis=2, concat_axis=1, tiled=True)
    screened_rho = right_columns(screened, lax.all_gather(halves, "row", axis=1, tiled=True))
    blocks = lax.all_to_all(rho, "row", split_axis=2, concat_axis=1, tiled=True)
    blocks = blocks.reshape(2, lax.axis_size("row"), owned, row_span)
    left_panel = lax.all_gather(blocks, "col", axis=2, tiled=True).reshape(2, NP, row_span)
    left_wide = left_panel.astype(jnp.float32)
    u_real = jnp.einsum(
        "ag,fgb->fab", left_wide[0], screened_rho[:, 0], precision=highest
    ) + jnp.einsum("ag,fgb->fab", left_wide[1], screened_rho[:, 1], precision=highest)
    u_imag = jnp.einsum(
        "ag,fgb->fab", left_wide[0], screened_rho[:, 1], precision=highest
    ) - jnp.einsum("ag,fgb->fab", left_wide[1], screened_rho[:, 0], precision=highest)
    partial_terms = jnp.stack([u_real, u_imag], axis=1) / math.sqrt(NG)
    summed = lax.psum(partial_terms, ("row", "col"))
    share_rows = NP // lax.axis_size(("row", "col"))
    return lax.dynamic_slice_in_dim(
        summed, lax.axis_index(("row", "col")) * share_rows, share_rows, 2
    )


def solution(mesh):
    return jax.shard_map(
        shards,
        mesh=mesh,
        in_specs=(P("kpt", ("row", "col"), None), P(), P(), P("kpt", None, "row", "col")),
        out_specs=P(None, None, ("kpt", "row", "col"), None),
        check_vma=False,
    )
```

profile of v0, /device:TPU:0, one launch (start us, length us, event | category | flops | bytes accessed | tf_op | source)
XLA Modules:
  0.0 687.3 jit_solution(8600309741713015094)
XLA Ops:
  15.1 7.5 %all-to-all-start = ((f32[384,2,1024]{2,1,0:T(2,128)}), f32[384,2,1024]{2,1,0:T(2,128)S(1)}, u32[]{:S(2)}, u32[]{:S(2)}) async-start(f32[384,2,1024]{2,1,0:T(2,128)} %reshape.35), calls=%async_computation | async-start | bytes 6291456 | tf_op jit(solution)/shard_map/all_to_all | solution.py:69
  22.7 59.1 %all-to-all-done = f32[384,2,1024]{2,1,0:T(2,128)S(1)} async-done(((f32[384,2,1024]{2,1,0:T(2,128)}), f32[384,2,1024]{2,1,0:T(2,128)S(1)}, u32[]{:S(2)}, u32[]{:S(2)}) %all-to-all-start) | async-done | bytes 3145760 | tf_op jit(solution)/shard_map/all_to_all | solution.py:69
  85.3 7.6 %reshape.36 = f32[768,32,32]{2,1,0:T(8,128)} reshape(f32[24,16,2,1024]{3,2,1,0:T(2,128)S(1)} %copy.71) | data formatting | bytes 6291456 | tf_op jit(solution)/shard_map/reshape | solution.py:23
  92.9 9.2 %copy.72 = f32[768,32,32]{0,2,1:T(8,128)S(1)} copy(f32[768,32,32]{2,1,0:T(8,128)} %reshape.36) | data formatting | bytes 6291456 | tf_op jit(solution)/shard_map/reshape | solution.py:23
  118.2 6.7 add_bitcast_fusion.1
  130.5 10.6 %copy.79 = f32[768,32,32]{2,1,0:T(8,128)} copy(f32[768,32,32]{0,1,2:T(8,128)S(1)} %subtract_bitcast_fusion.1) | data formatting | bytes 6291456 | tf_op jit(solution)/shard_map/sub | solution.py:29
  141.1 9.4 %reshape.38 = f32[24,32,1024]{2,1,0:T(8,128)S(1)} reshape(f32[768,32,32]{2,1,0:T(8,128)} %copy.79) | data formatting | bytes 6291456 | tf_op jit(solution)/shard_map/reshape | solution.py:32
  155.9 11.4 %copy.76 = f32[768,32,32]{2,1,0:T(8,128)} copy(f32[768,32,32]{0,1,2:T(8,128)} %add_bitcast_fusion.1) | data formatting | bytes 6291456 | tf_op jit(solution)/shard_map/add | solution.py:26
  167.3 10.7 %reshape.37 = f32[24,32,1024]{2,1,0:T(8,128)} reshape(f32[768,32,32]{2,1,0:T(8,128)} %copy.76) | data formatting | bytes 6291456 | tf_op jit(solution)/shard_map/reshape | solution.py:32
  178.0 5.9 fusion.69
  184.0 5.5 subtract_bitcast_fusion
  189.5 5.6 add_bitcast_fusion
  195.1 10.3 %copy.89 = f32[24,32,1024]{0,2,1:T(8,128)} copy(f32[24,32,1024]{2,1,0:T(8,128)} %add_bitcast_fusion) | data formatting | bytes 6291456 | tf_op jit(solution)/shard_map/reshape | solution.py:74
  205.4 8.6 %copy.90 = f32[24,32,1024]{0,2,1:T(8,128)} copy(f32[24,32,1024]{2,1,0:T(8,128)S(1)} %copy-done.2) | data formatting | bytes 6291456 | tf_op jit(solution)/shard_map/reshape | solution.py:75
  214.0 33.6 %gather_fusion = f32[8192,24]{1,0:T(8,128)} fusion(f32[24,32768]{0,1:T(8,128)} %bitcast.144, s32[8192]{0:T(1024)S(1)} %fusion.57), kind=kCustom, calls=%fused_computation.clone | custom fusion | bytes 1605632 | tf_op jit(solution)/shard_map/jit(_take)/gather | solution.py:74
  247.6 33.6 %gather_fusion.1 = f32[8192,24]{1,0:T(8,128)} fusion(f32[24,32768]{0,1:T(8,128)} %bitcast.143, s32[8192]{0:T(1024)S(1)} %fusion.57), kind=kCustom, calls=%fused_computation.1.clone | custom fusion | bytes 1605632 | tf_op jit(solution)/shard_map/jit(_take)/gather | solution.py:75
  281.3 7.2 %fusion.30 = (bf16[1,24,8192]{1,2,0:T(8,128)(2,1)S(1)}, bf16[1,24,8192]{1,2,0:T(8,128)(2,1)S(1)}) fusion(f32[8192,24]{1,0:T(8,128)} %gather_fusion, pred[8192]{0:T(1024)(128)(4,1)S(1)} %compare_and_fusion, f32[8192,24]{1,0:T(8,128)} %gather_fusion.1), kind=kLoop, calls=%fused_computation.43 | loop fusion | flops 1179648 | bytes 2367488 | tf_op jit(solution)/shard_map/stack | solution.py:76
  289.4 35.5 %copy.108 = bf16[2,24,8192]{1,0,2:T(2,128)(2,1)} copy(bf16[2,24,8192]{1,2,0:T(8,128)(2,1)S(1)} %pad_maximum_fusion) | data formatting | bytes 1572864 | tf_op jit(solution)/shard_map/stack | solution.py:76
  324.9 6.6 reshape.71
  331.5 35.8 %all_to_all.48 = bf16[8,2,24576]{2,1,0:T(2,128)(2,1)S(1)} all-to-all(bf16[8,2,24576]{2,1,0:T(2,128)(2,1)S(1)} %reshape.71), channel_id=1, replica_groups=mesh['kpt'=2,'row'=8,'col'=2] {'row'}, dimensions={0} | all-to-all | bytes 1572864 | tf_op jit(solution)/shard_map/all_to_all | solution.py:80
  367.3 6.9 %reshape.72 = bf16[8192,2,24]{2,1,0:T(2,128)(2,1)} reshape(bf16[8,2,24576]{2,1,0:T(2,128)(2,1)S(1)} %all_to_all.48) | data formatting | bytes 1572864
  374.3 10.3 %copy.87 = bf16[2,24,8,1024]{3,1,2,0:T(8,128)(2,1)} copy(bf16[2,24,8,1024]{1,0,3,2:T(2,128)(2,1)} %bitcast.145) | data formatting | bytes 1572864 | tf_op jit(solution)/shard_map/all_to_all | solution.py:80
  384.6 10.2 %copy.109 = bf16[2,24,8192]{1,0,2:T(2,128)(2,1)} copy(bf16[2,24,8192]{1,2,0:T(8,128)(2,1)} %copy-done) | data formatting | bytes 1572864 | tf_op jit(solution)/shard_map/stack | solution.py:76
  394.8 7.0 %reshape.73 = bf16[2,2,98304]{2,1,0:T(2,128)(2,1)S(1)} reshape(bf16[8192,2,24]{2,1,0:T(2,128)(2,1)} %bitcast.147) | data formatting | bytes 1572864
  406.2 7.3 %reshape.74 = bf16[8192,2,24]{2,1,0:T(2,128)(2,1)} reshape(bf16[2,2,98304]{2,1,0:T(2,128)(2,1)S(1)} %all_to_all.49) | data formatting | bytes 1572864
  413.6 9.5 %copy.83 = bf16[2,24,2,4096]{3,1,2,0:T(8,128)(2,1)} copy(bf16[2,24,2,4096]{1,0,3,2:T(2,128)(2,1)} %bitcast.146) | data formatting | bytes 1572864 | tf_op jit(solution)/shard_map/all_to_all | solution.py:78
  424.7 96.3 %all-gather.3.cloned.1.call-done = bf16[2,384,4096]{2,1,0:T(8,128)(2,1)} async-done(((bf16[2,48,4096]{2,1,0:T(8,128)(2,1)}), bf16[2,384,4096]{2,1,0:T(8,128)(2,1)}) %all-gather.3.cloned.1.call-update) | async-done | bytes 6291472 | tf_op jit(solution)/shard_map/all_gather | solution.py:79
  521.0 11.4 %fusion = f32[384,2,1024]{2,0,1:T(8,128)S(1)} fusion(bf16[2,2,1024,4096]{3,2,1,0:T(8,128)(2,1)} %param.9, bf16[2,384,4096]{2,1,0:T(8,128)(2,1)} %all-gather.3.cloned.1.call-done), kind=kOutput, calls=%fused_computation.2 | convolution fusion | flops 6442450944 | bytes 23068672 | tf_op jit(solution)/shard_map/fgh,bh->fgb/dot_general | solution.py:53
  532.4 11.2 %fusion.39 = f32[384,2,1024]{2,0,1:T(8,128)S(1)} fusion(f32[384,2,1024]{2,0,1:T(8,128)S(1)} %fusion, bf16[2,2,1024,4096]{3,2,1,0:T(8,128)(2,1)} %param.9, bf16[2,384,4096]{2,1,0:T(8,128)(2,1)} %all-gather.3.cloned.1.call-done), kind=kOutput, calls=%fused_computation.47 | convolution fusion | flops 6443237376 | bytes 26214400 | tf_op jit(solution)/shard_map/fgh,bh->fgb/dot_general | solution.py:52
  548.9 12.6 %fusion.2 = f32[384,2,1024]{2,0,1:T(8,128)} fusion(bf16[2,2,1024,4096]{3,2,1,0:T(8,128)(2,1)} %param.9, bf16[2,384,4096]{2,1,0:T(8,128)(2,1)} %all-gather.3.cloned.1.call-done), kind=kOutput, calls=%fused_computation.4 | convolution fusion | flops 6442450944 | bytes 23068672 | tf_op jit(solution)/shard_map/fgh,bh->fgb/dot_general | solution.py:51
  561.5 12.1 %fusion.36 = f32[384,2,1024]{2,0,1:T(8,128)S(1)} fusion(f32[384,2,1024]{2,0,1:T(8,128)} %fusion.2, bf16[2,2,1024,4096]{3,2,1,0:T(8,128)(2,1)} %param.9, bf16[2,384,4096]{2,1,0:T(8,128)(2,1)} %all-gather.3.cloned.1.call-done), kind=kOutput, calls=%fused_computation.46 | convolution fusion | flops 6443237376 | bytes 26214400 | tf_op jit(solution)/shard_map/fgh,bh->fgb/dot_general | solution.py:50
  580.6 97.4 %all-reduce.2.cloned.1.call-done = f32[2,2,384,384]{2,3,0,1:T(8,128)} async-done(((f32[2,2,384,384]{2,3,0,1:T(8,128)}), f32[2,2,384,384]{2,3,0,1:T(8,128)}) %all-reduce.2.cloned.1.call-update) | async-done | bytes 2359312 | tf_op jit(solution)/shard_map/psum | solution.py:91
  (42 shorter events, 60.9 us)
Async XLA Ops:
  15.1 7.6 %copy-start.4 = (s32[8192]{0:T(1024)S(1)}, s32[8192]{0:T(1024)}, u32[]{:S(2)}) copy-start(s32[8192]{0:T(1024)} %param.8) | copy-start | bytes 98308
  15.1 66.8 %all-to-all-start = ((f32[384,2,1024]{2,1,0:T(2,128)}), f32[384,2,1024]{2,1,0:T(2,128)S(1)}, u32[]{:S(2)}, u32[]{:S(2)}) async-start(f32[384,2,1024]{2,1,0:T(2,128)} %reshape.35), calls=%async_computation | async-start | bytes 6291456 | tf_op jit(solution)/shard_map/all_to_all | solution.py:69
  22.6 400.5 %all-gather.5.cloned.1.call-start = ((), (), s32[]{:S(2)}) async-start(), calls=%async_computation.4 | async-start | bytes 2359296 | tf_op jit(solution)/shard_map/all_gather | solution.py:82
  178.0 6.0 copy-start.1
  178.0 6.0 copy-start.3
  195.1 10.3 %copy-start.2 = (f32[24,32,1024]{2,1,0:T(8,128)S(1)}, f32[24,32,1024]{2,1,0:T(8,128)}, u32[]{:S(2)}) copy-start(f32[24,32,1024]{2,1,0:T(8,128)} %subtract_bitcast_fusion) | copy-start | bytes 9437188
  289.4 35.5 %copy-start = (bf16[2,24,8192]{1,2,0:T(8,128)(2,1)}, bf16[2,24,8192]{1,2,0:T(8,128)(2,1)S(1)}, u32[]{:S(2)}) copy-start(bf16[2,24,8192]{1,2,0:T(8,128)(2,1)S(1)} %pad_maximum_fusion) | copy-start | bytes 2359300
  384.6 136.4 %all-gather.3.cloned.1.call-start = ((), (), s32[]{:S(2)}) async-start(), calls=%async_computation.3 | async-start | bytes 7077888 | tf_op jit(solution)/shard_map/all_gather | solution.py:79
  423.1 254.9 %all-reduce.2.cloned.1.call-start = ((), (), s32[]{:S(2)}) async-start(), calls=%async_computation.5 | async-start | bytes 4718592 | tf_op jit(solution)/shard_map/psum | solution.py:91
Sparse Core Ops, SparseCore 0:
  384.7 8.8 all-gather.4
  423.2 97.7 all-gather.2
  580.7 97.1 all-reduce.1
where the time goes:
time: 696 us; the launch traced here: 687 us
  waiting for transfers between devices  253 us (36%)
  local copies, waits for them, and re-layouts  251 us (36%)
  matrix products  112 us (16%)
  blocking collectives  40.2 us (6%)
  between operations  13.7 us (2%)
  other arithmetic  9.75 us (1%)
  starting transfers between devices  7.67 us (1%)
    psum x1, waiting for transfers between devices, shards(): summed = lax.psum(partial_terms, ('row', 'col'))  97.4 us
    all_gather x1, waiting for transfers between devices, shards(): lax.all_gather(halves, 'row', axis=1, tiled=True)  96.3 us
    all_to_all x1, waiting for transfers between devices, shards(): lax.all_to_all(density, ('row', 'col'), split_axis=0, concat_axis=1, tile...  59.1 us
    another operation x2, local copies, waits for them, and re-layouts, shards(): rho = jnp.stack([rho_real, rho_imag], axis=0).astype(jnp.bfloat16)  45.7 us
    all_to_all x1, blocking collectives, shards(): blocks = lax.all_to_all(rho, 'row', split_axis=2, concat_axis=1, tiled=True)  35.8 us
    gather x1, local copies, waits for them, and re-layouts, shards(): jnp.take(imag_part.reshape(owned, -1), gmap, axis=1) * norm_factor  33.6 us
    gather x1, local copies, waits for them, and re-layouts, shards(): jnp.take(real_part.reshape(owned, -1), gmap, axis=1) * norm_factor  33.6 us
    unnamed x15, local copies, waits for them, and re-layouts  29 us
  transfers between devices with their start and end apart: 4, of which 3 were waited for; matrix products, arithmetic and copies ran while one was open for 5% of the time, Pallas kernels for 0%

commit v1 on v0

--- a/solution.py
+++ b/solution.py
@@ -88,7 +88,8 @@
         "ag,fgb->fab", left_wide[0], screened_rho[:, 1], precision=highest
     ) - jnp.einsum("ag,fgb->fab", left_wide[1], screened_rho[:, 0], precision=highest)
     partial_terms = jnp.stack([u_real, u_imag], axis=1) / math.sqrt(NG)
-    summed = lax.psum(partial_terms, ("row", "col"))
+    pieces = lax.all_gather(partial_terms, ("row", "col"), axis=0, tiled=False)
+    summed = pieces.sum(axis=0)
     share_rows = NP // lax.axis_size(("row", "col"))
     return lax.dynamic_slice_in_dim(
         summed, lax.axis_index(("row", "col")) * share_rows, share_rows, 2

time: 696 us -> 807 us (1.16)
  waiting for transfers between devices: 253 us -> 342 us
  other arithmetic: 9.75 us -> 21.4 us
    all_gather x0 -> x1, waiting for transfers between devices: none -> 186 us  [shards(): pieces = lax.all_gather(partial_terms, ('row', 'col'), axis=0, tiled=False)]
    psum x1 -> x0, waiting for transfers between devices: 97.4 us -> none  [shards(): summed = lax.psum(partial_terms, ('row', 'col'))]
    reduce_sum x0 -> x1, other arithmetic: none -> 13.5 us  [shards(): summed = pieces.sum(axis=0)]
    unnamed x15 -> x17, local copies, waits for them, and re-layouts: 29 us -> 30.6 us
  transfers between devices with their start and end apart: 4 -> 4, of which waited for: 3 -> 3; matrix products, arithmetic and copies ran while one was open for 5% -> 4% of each run, Pallas kernels for 0% -> 0%
where the time goes in v1:
time: 807 us; the launch traced here: 798 us
  waiting for transfers between devices  342 us (42%)
  local copies, waits for them, and re-layouts  256 us (32%)
  matrix products  118 us (15%)
  blocking collectives  40.2 us (5%)
  other arithmetic  21.4 us (3%)
  between operations  13.6 us (2%)
    all_gather x1, waiting for transfers between devices, shards(): pieces = lax.all_gather(partial_terms, ('row', 'col'), axis=0, tiled=False)  186 us
    all_gather x1, waiting for transfers between devices, shards(): lax.all_gather(halves, 'row', axis=1, tiled=True)  96.3 us
    all_to_all x1, waiting for transfers between devices, shards(): lax.all_to_all(density, ('row', 'col'), split_axis=0, concat_axis=1, tile...  59.1 us
    another operation x2, local copies, waits for them, and re-layouts, shards(): rho = jnp.stack([rho_real, rho_imag], axis=0).astype(jnp.bfloat16)  46.1 us
    all_to_all x1, blocking collectives, shards(): blocks = lax.all_to_all(rho, 'row', split_axis=2, concat_axis=1, tiled=True)  35.8 us
    gather x1, local copies, waits for them, and re-layouts, shards(): jnp.take(imag_part.reshape(owned, -1), gmap, axis=1) * norm_factor  33.5 us
    gather x1, local copies, waits for them, and re-layouts, shards(): jnp.take(real_part.reshape(owned, -1), gmap, axis=1) * norm_factor  33.5 us
    unnamed x17, local copies, waits for them, and re-layouts  30.6 us
  transfers between devices with their start and end apart: 4, of which 3 were waited for; matrix products, arithmetic and copies ran while one was open for 4% of the time, Pallas kernels for 0%

profile of v1, /device:TPU:0, one launch (start us, length us, event | category | flops | bytes accessed | tf_op | source)
XLA Modules:
  0.0 798.1 jit_solution(6940244225572223002)
XLA Ops:
  15.1 7.5 all-to-all-start
  22.7 59.1 %all-to-all-done = f32[384,2,1024]{2,1,0:T(2,128)S(1)} async-done(((f32[384,2,1024]{2,1,0:T(2,128)}), f32[384,2,1024]{2,1,0:T(2,128)S(1)}, u32[]{:S(2)}, u32[]{:S(2)}) %all-to-all-start) | async-done | bytes 3145760 | tf_op jit(solution)/shard_map/all_to_all | solution.py:69
  85.3 7.5 reshape.67
  92.8 9.2 %copy.71 = f32[768,32,32]{0,2,1:T(8,128)S(1)} copy(f32[768,32,32]{2,1,0:T(8,128)} %reshape.67) | data formatting | bytes 6291456 | tf_op jit(solution)/shard_map/reshape | solution.py:23
  116.4 6.7 fusion.24
  123.1 6.7 subtract_bitcast_fusion.1
  129.8 11.4 %copy.78 = f32[768,32,32]{2,1,0:T(8,128)} copy(f32[768,32,32]{0,1,2:T(8,128)} %subtract_bitcast_fusion.1) | data formatting | bytes 6291456 | tf_op jit(solution)/shard_map/sub | solution.py:29
  141.2 10.9 %reshape.69 = f32[24,32,1024]{2,1,0:T(8,128)} reshape(f32[768,32,32]{2,1,0:T(8,128)} %copy.78) | data formatting | bytes 6291456 | tf_op jit(solution)/shard_map/reshape | solution.py:32
  152.1 7.5 fusion.66
  159.7 6.7 add_bitcast_fusion.1
  166.4 11.4 %copy.75 = f32[768,32,32]{2,1,0:T(8,128)} copy(f32[768,32,32]{0,1,2:T(8,128)} %add_bitcast_fusion.1) | data formatting | bytes 6291456 | tf_op jit(solution)/shard_map/add | solution.py:26
  177.8 9.5 %reshape.68 = f32[24,32,1024]{2,1,0:T(8,128)S(1)} reshape(f32[768,32,32]{2,1,0:T(8,128)} %copy.75) | data formatting | bytes 6291456 | tf_op jit(solution)/shard_map/reshape | solution.py:32
  198.4 10.2 %copy.91 = f32[24,32,1024]{0,2,1:T(8,128)} copy(f32[24,32,1024]{2,1,0:T(8,128)} %subtract_bitcast_fusion) | data formatting | bytes 6291456 | tf_op jit(solution)/shard_map/reshape | solution.py:75
  214.6 10.1 %copy.90 = f32[24,32,1024]{0,2,1:T(8,128)} copy(f32[24,32,1024]{2,1,0:T(8,128)} %add_bitcast_fusion) | data formatting | bytes 6291456 | tf_op jit(solution)/shard_map/reshape | solution.py:74
  224.7 33.5 %gather_fusion.1 = f32[8192,24]{1,0:T(8,128)} fusion(f32[24,32768]{0,1:T(8,128)} %bitcast.143, s32[8192]{0:T(1024)S(1)} %fusion.57), kind=kCustom, calls=%fused_computation.1.clone | custom fusion | bytes 1605632 | tf_op jit(solution)/shard_map/jit(_take)/gather | solution.py:75
  258.2 33.5 %gather_fusion = f32[8192,24]{1,0:T(8,128)} fusion(f32[24,32768]{0,1:T(8,128)} %bitcast.144, s32[8192]{0:T(1024)S(1)} %fusion.57), kind=kCustom, calls=%fused_computation.clone | custom fusion | bytes 1605632 | tf_op jit(solution)/shard_map/jit(_take)/gather | solution.py:74
  291.7 6.8 fusion.30
  299.4 35.9 %copy.111 = bf16[2,24,8192]{1,0,2:T(2,128)(2,1)} copy(bf16[2,24,8192]{1,2,0:T(8,128)(2,1)S(1)} %pad_maximum_fusion) | data formatting | bytes 1572864 | tf_op jit(solution)/shard_map/stack | solution.py:76
  341.9 35.8 %all_to_all.48 = bf16[8,2,24576]{2,1,0:T(2,128)(2,1)S(1)} all-to-all(bf16[8,2,24576]{2,1,0:T(2,128)(2,1)S(1)} %reshape.102), channel_id=1, replica_groups=mesh['kpt'=2,'row'=8,'col'=2] {'row'}, dimensions={0} | all-to-all | bytes 1572864 | tf_op jit(solution)/shard_map/all_to_all | solution.py:80
  377.7 6.9 reshape.103
  384.6 10.3 %copy.86 = bf16[2,24,8,1024]{3,1,2,0:T(8,128)(2,1)} copy(bf16[2,24,8,1024]{1,0,3,2:T(2,128)(2,1)} %bitcast.145) | data formatting | bytes 1572864 | tf_op jit(solution)/shard_map/all_to_all | solution.py:80
  395.0 10.2 %copy.112 = bf16[2,24,8192]{1,0,2:T(2,128)(2,1)} copy(bf16[2,24,8192]{1,2,0:T(8,128)(2,1)} %copy-done) | data formatting | bytes 1572864 | tf_op jit(solution)/shard_map/stack | solution.py:76
  405.2 7.0 reshape.104
  416.6 7.3 reshape.105
  423.9 9.4 %copy.82 = bf16[2,24,2,4096]{3,1,2,0:T(8,128)(2,1)} copy(bf16[2,24,2,4096]{1,0,3,2:T(2,128)(2,1)} %bitcast.146) | data formatting | bytes 1572864 | tf_op jit(solution)/shard_map/all_to_all | solution.py:78
  435.0 96.3 %all-gather.4.cloned.1.call-done = bf16[2,384,4096]{2,1,0:T(8,128)(2,1)} async-done(((bf16[2,48,4096]{2,1,0:T(8,128)(2,1)}), bf16[2,384,4096]{2,1,0:T(8,128)(2,1)}) %all-gather.4.cloned.1.call-update) | async-done | bytes 6291472 | tf_op jit(solution)/shard_map/all_gather | solution.py:79
  531.3 11.4 %fusion = f32[384,2,1024]{2,0,1:T(8,128)S(1)} fusion(bf16[2,2,1024,4096]{3,2,1,0:T(8,128)(2,1)} %param.9, bf16[2,384,4096]{2,1,0:T(8,128)(2,1)} %all-gather.4.cloned.1.call-done), kind=kOutput, calls=%fused_computation.2 | convolution fusion | flops 6442450944 | bytes 23068672 | tf_op jit(solution)/shard_map/fgh,bh->fgb/dot_general | solution.py:53
  542.7 11.2 %fusion.39 = f32[384,2,1024]{2,0,1:T(8,128)S(1)} fusion(f32[384,2,1024]{2,0,1:T(8,128)S(1)} %fusion, bf16[2,2,1024,4096]{3,2,1,0:T(8,128)(2,1)} %param.9, bf16[2,384,4096]{2,1,0:T(8,128)(2,1)} %all-gather.4.cloned.1.call-done), kind=kOutput, calls=%fused_computation.47 | convolution fusion | flops 6443237376 | bytes 26214400 | tf_op jit(solution)/shard_map/fgh,bh->fgb/dot_general | solution.py:52
  559.2 12.6 %fusion.2 = f32[384,2,1024]{2,0,1:T(8,128)} fusion(bf16[2,2,1024,4096]{3,2,1,0:T(8,128)(2,1)} %param.9, bf16[2,384,4096]{2,1,0:T(8,128)(2,1)} %all-gather.4.cloned.1.call-done), kind=kOutput, calls=%fused_computation.4 | convolution fusion | flops 6442450944 | bytes 23068672 | tf_op jit(solution)/shard_map/fgh,bh->fgb/dot_general | solution.py:51
  571.8 11.8 %fusion.36 = f32[384,2,1024]{2,0,1:T(8,128)S(1)} fusion(f32[384,2,1024]{2,0,1:T(8,128)} %fusion.2, bf16[2,2,1024,4096]{3,2,1,0:T(8,128)(2,1)} %param.9, bf16[2,384,4096]{2,1,0:T(8,128)(2,1)} %all-gather.4.cloned.1.call-done), kind=kOutput, calls=%fused_computation.46 | convolution fusion | flops 6443237376 | bytes 26214400 | tf_op jit(solution)/shard_map/fgh,bh->fgb/dot_general | solution.py:50
  591.1 186.1 %all-gather.8.cloned.1.call-done = f32[16,2,2,384,384]{4,3,2,1,0:T(8,128)} async-done(((f32[1,2,2,384,384]{4,3,2,1,0:T(8,128)}), f32[16,2,2,384,384]{4,3,2,1,0:T(8,128)}) %all-gather.8.cloned.1.call-update) | async-done | bytes 37748752 | tf_op jit(solution)/shard_map/all_gather | solution.py:91
  777.2 13.5 %reduce_sum.9 = f32[2,2,384,384]{3,2,1,0:T(8,128)S(1)} reduce(f32[16,2,2,384,384]{4,3,2,1,0:T(8,128)} %all-gather.8.cloned.1.call-done, f32[]{:T(128)} %constant.46.clone.1), dimensions={0}, to_apply=%region_0.2 | reduce | flops 8847360 | bytes 40108036 | tf_op jit(solution)/shard_map/reduce_sum | solution.py:92
  (45 shorter events, 70.5 us)
Async XLA Ops:
  15.1 7.6 copy-start.5
  15.1 66.8 %all-to-all-start = ((f32[384,2,1024]{2,1,0:T(2,128)}), f32[384,2,1024]{2,1,0:T(2,128)S(1)}, u32[]{:S(2)}, u32[]{:S(2)}) async-start(f32[384,2,1024]{2,1,0:T(2,128)} %reshape.66), calls=%async_computation | async-start | bytes 6291456 | tf_op jit(solution)/shard_map/all_to_all | solution.py:69
  22.6 410.8 %all-gather.6.cloned.1.call-start = ((), (), s32[]{:S(2)}) async-start(), calls=%async_computation.4 | async-start | bytes 2359296 | tf_op jit(solution)/shard_map/all_gather | solution.py:82
  102.0 1.6 copy-start.1
  152.1 7.6 copy-start.3
  187.3 5.5 copy-start.4
  198.4 10.2 %copy-start.2 = (f32[24,32,1024]{2,1,0:T(8,128)S(1)}, f32[24,32,1024]{2,1,0:T(8,128)}, u32[]{:S(2)}) copy-start(f32[24,32,1024]{2,1,0:T(8,128)} %reshape.69) | copy-start | bytes 9437188
  299.4 35.9 %copy-start = (bf16[2,24,8192]{1,2,0:T(8,128)(2,1)}, bf16[2,24,8192]{1,2,0:T(8,128)(2,1)S(1)}, u32[]{:S(2)}) copy-start(bf16[2,24,8192]{1,2,0:T(8,128)(2,1)S(1)} %pad_maximum_fusion) | copy-start | bytes 2359300
  395.0 136.3 %all-gather.4.cloned.1.call-start = ((), (), s32[]{:S(2)}) async-start(), calls=%async_computation.3 | async-start | bytes 7077888 | tf_op jit(solution)/shard_map/all_gather | solution.py:79
  433.4 343.8 %all-gather.8.cloned.1.call-start = ((), (), s32[]{:S(2)}) async-start(), calls=%async_computation.5 | async-start | bytes 40108032 | tf_op jit(solution)/shard_map/all_gather | solution.py:91
Sparse Core Ops, SparseCore 0:
  395.1 8.8 all-gather.5
  433.5 97.7 all-gather.3
  591.2 185.9 all-gather.7
